TPU v7x, 32 devices: a whole 2x2x4 slice. The times are simulated.
32 devices in a mesh: tp: 4 (over y, x), dp: 8 (over z, core).
Axes of the slice: x: 2, y: 2, z: 4, core: 2. Of those that a mesh axis runs over, the one named last changes fastest.
Arguments:
- activations: bfloat16 [2, 8192, 8192], P(None, 'dp', 'tp'), may hold values from -72 to 72
- out_grads: bfloat16 [2, 8192, 2048], P(None, 'dp'), may hold values from -2 to 2
- master: float32 [8192, 2, 2048], P(('tp', 'dp')), may hold values from -1.2 to 1.2
- first_moment: float32 [8192, 2, 2048], P(('tp', 'dp')), may hold values from -1.8 to 1.8
- second_moment: float32 [8192, 2, 2048], P(('tp', 'dp')), may hold values from 0.01 to 1
Outputs:
- new_master: float32 [8192, 2, 2048], P(('tp', 'dp'))
- new_first: float32 [8192, 2, 2048], P(('tp', 'dp'))
- new_second: float32 [8192, 2, 2048], P(('tp', 'dp'))
- weights: bfloat16 [8192, 2, 2048], P('tp')
All inputs are finite; a program needn't handle non-finite values.
Results may differ from a plain program's by a relative error of at most 0.0004.
Values may be sent and summed in bfloat16 or wider, within the bound.
A program may use at most 192 MiB of HBM per device.

v0:
```python
import math
import jax
import jax.numpy as jnp
from jax import lax
from jax.sharding import PartitionSpec as P

beta_first = 0.9
beta_second = 0.95
first_fix = 1.0 - 0.9**10
second_fix = 1.0 - 0.95**10
learn_rate = 0.01
decay_rate = 0.1
epsilon = 1e-08
limit_scale = 2.0


def reduce_rows(layer_acts, layer_grads):
    grad_own = lax.psum_scatter(
        jnp.einsum("ltr,ltc->rlc", layer_acts, layer_grads, preferred_element_type=jnp.float32),
        "dp",
        scatter_dimension=0,
        tiled=True,
    )
    partial_value = jnp.sum(grad_own * grad_own)
    return (grad_own, partial_value)


def adam_update(grad_own, master, first_moment, second_moment, clip_factor):
    clipped = clip_factor * grad_own
    new_first = beta_first * first_moment + (1.0 - beta_first) * clipped
    new_second = beta_second * second_moment + (1.0 - beta_second) * clipped * clipped
    step_dir = new_first / first_fix / (jnp.sqrt(new_second / second_fix) + epsilon)
    new_master = master - learn_rate * (step_dir + decay_rate * master)
    return (new_master, new_first, new_second)


def on_device(activations, out_grads, master, first_moment, second_moment):
    own_rows = master.shape[0]
    grad_own, layer_sum = reduce_rows(activations, out_grads)
    sum_squares = lax.psum(layer_sum, ("tp", "dp"))
    entries = (
        own_rows * lax.axis_size("tp") * lax.axis_size("dp") * master.shape[1] * master.shape[2]
    )
    limit = limit_scale * math.sqrt(entries)
    clip_factor = limit / jnp.maximum(jnp.sqrt(sum_squares), limit)
    new_master, new_first, new_second = adam_update(
        grad_own, master, first_moment, second_moment, clip_factor
    )
    rounded = new_master.astype(jnp.bfloat16)
    tp_rows = lax.all_gather(rounded, "dp", axis=0, tiled=True)
    return (new_master, new_first, new_second, tp_rows)


def solution(mesh):
    return jax.shard_map(
        on_device,
        mesh=mesh,
        in_specs=(
            P(None, "dp", "tp"),
            P(None, "dp", None),
            P(("tp", "dp"), None, None),
            P(("tp", "dp"), None, None),
            P(("tp", "dp"), None, None),
        ),
        out_specs=(
            P(("tp", "dp"), None, None),
            P(("tp", "dp"), None, None),
            P(("tp", "dp"), None, None),
            P("tp", None, None),
        ),
        check_vma=False,
    )
```

profile of v0, /device:TPU:0, one launch (start us, length us, event | category | flops | bytes accessed | tf_op | source)
XLA Modules:
  0.0 623.6 jit_solution(12652880110053405186)
XLA Ops:
  7.2 0.0 reduce-scatter.2.cloned.1.call-start
  7.2 25.6 %convolution_bitcast_fusion = f32[2048,2,2048]{0,2,1:T(8,128)} fusion(bf16[2,1024,2048]{2,1,0:T(8,128)(2,1)} %param.6, bf16[2,1024,2048]{2,1,0:T(8,128)(2,1)} %param.5), kind=kOutput, calls=%fused_computation | convolution fusion | flops 17179869184 | bytes 50331648 | tf_op jit(solution)/shard_map/ltr,ltc->rlc/dot_general | solution.py:19
  32.9 0.0 reduce-scatter.2.cloned.1.call-update
  32.9 0.0 all-gather.2.cloned.1.call-start
  32.9 7.2 %copy.13 = f32[256,2,2048]{0,2,1:T(8,128)} copy(f32[256,2,2048]{2,1,0:T(2,128)} %param.7) | data formatting | bytes 8388608 | tf_op args[2]
  40.1 7.2 %copy.9 = f32[256,2,2048]{0,2,1:T(8,128)} copy(f32[256,2,2048]{2,1,0:T(2,128)} %param.8) | data formatting | bytes 8388608 | tf_op args[3]
  47.4 313.8 %reduce-scatter.2.cloned.1.call-done = f32[256,2,2048]{0,2,1:T(8,128)} async-done(((f32[2048,2,2048]{0,2,1:T(8,128)}), f32[256,2,2048]{0,2,1:T(8,128)}) %reduce-scatter.2.cloned.1.call-update) | async-done | bytes 4194320 | tf_op jit(solution)/shard_map/reduce_scatter | solution.py:18
  361.2 3.9 multiply_reduce_fusion
  365.1 7.2 %copy.11 = f32[256,2,2048]{0,2,1:T(8,128)} copy(f32[256,2,2048]{2,1,0:T(2,128)} %param.9) | data formatting | bytes 8388608 | tf_op args[4]
  372.3 37.9 %psum.7 = f32[]{:T(128)} all-reduce(f32[]{:T(128)} %multiply_reduce_fusion), channel_id=1, replica_groups=mesh['tp'=4,'dp'=8] {'tp','dp'}, use_global_device_ids=true, to_apply=%region_2.0 | all-reduce | flops 1 | bytes 8 | tf_op jit(solution)/shard_map/psum | solution.py:40
  411.0 11.7 %fusion.1 = (bf16[256,2,2048]{0,2,1:T(8,128)(2,1)}, f32[256,2,2048]{0,2,1:T(8,128)}, f32[256,2,2048]{0,2,1:T(8,128)}, f32[256,2,2048]{0,2,1:T(8,128)}) fusion(f32[256,2,2048]{0,2,1:T(8,128)} %copy.13, f32[256,2,2048]{0,2,1:T(8,128)} %reduce-scatter.2.cloned.1.call-done, f32[]{:T(128)S(6)} %div.18, f32[256,2,2048]{0,2,1:T(8,128)} %copy.9, f32[256,2,2048]{0,2,1:T(8,128)} %copy.11), kind=kLoop, calls=%fused_computation.6 | loop fusion | flops 17825792 | bytes 31457284 | tf_op jit(solution)/shard_map/convert_element_type | solution.py:49
  422.7 0.0 all-gather.2.cloned.1.call-update
  422.7 7.3 %copy.14 = f32[256,2,2048]{2,1,0:T(2,128)} copy(f32[256,2,2048]{0,2,1:T(8,128)} %get-tuple-element.9) | data formatting | bytes 8388608
  430.0 7.7 %copy.15 = f32[256,2,2048]{2,1,0:T(2,128)} copy(f32[256,2,2048]{0,2,1:T(8,128)} %get-tuple-element.10) | data formatting | bytes 8388608
  437.7 7.3 %copy.16 = f32[256,2,2048]{2,1,0:T(2,128)} copy(f32[256,2,2048]{0,2,1:T(8,128)} %get-tuple-element.11) | data formatting | bytes 8388608
  445.0 130.3 %all-gather.2.cloned.1.call-done = bf16[2048,2,2048]{0,2,1:T(8,128)(2,1)} async-done(((bf16[256,2,2048]{0,2,1:T(8,128)(2,1)}), bf16[2048,2,2048]{0,2,1:T(8,128)(2,1)}) %all-gather.2.cloned.1.call-update) | async-done | bytes 16777232 | tf_op jit(solution)/shard_map/all_gather | solution.py:50
  575.3 41.5 %copy.17 = bf16[2048,2,2048]{2,1,0:T(2,128)(2,1)} copy(bf16[2048,2,2048]{0,2,1:T(8,128)(2,1)} %all-gather.2.cloned.1.call-done) | data formatting | bytes 33554432
Async XLA Ops:
  7.2 354.1 %reduce-scatter.2.cloned.1.call-start = ((), (), s32[]{:S(2)}) async-start(), calls=%async_computation.1 | async-start | bytes 37748736 | tf_op jit(solution)/shard_map/reduce_scatter | solution.py:18
  32.9 542.4 %all-gather.2.cloned.1.call-start = ((), (), s32[]{:S(2)}) async-start(), calls=%async_computation.2 | async-start | bytes 18874368 | tf_op jit(solution)/shard_map/all_gather | solution.py:50
Sparse Core Ops, SparseCore 0:
  33.0 328.1 reduce-scatter.1
  422.8 152.4 all-gather.1
where the time goes:
time: 626 us; the launch traced here: 624 us
  waiting for transfers between devices  444 us (71%)
  local copies, waits for them, and re-layouts  85.4 us (14%)
  blocking collectives  37.9 us (6%)
  matrix products  25.6 us (4%)
  other arithmetic  15.6 us (2%)
  between operations  14.8 us (2%)
    reduce_scatter x1, waiting for transfers between devices, reduce_rows(): lax.psum_scatter(jnp.einsum('ltr,ltc->rlc', layer_acts, layer_grads, pref...  314 us
    all_gather x1, waiting for transfers between devices, on_device(): tp_rows = lax.all_gather(rounded, 'dp', axis=0, tiled=True)  130 us
    unnamed x7, local copies, waits for them, and re-layouts  85.4 us
    psum x1, blocking collectives, on_device(): sum_squares = lax.psum(layer_sum, ('tp', 'dp'))  37.9 us
    dot_general x1, matrix products, reduce_rows(): jnp.einsum('ltr,ltc->rlc', layer_acts, layer_grads, preferred_element_typ...  25.6 us
  transfers between devices with their start and end apart: 2, of which 2 were waited for; matrix products, arithmetic and copies ran while one was open for 6% of the time, Pallas kernels for 0%

commit v1 on v0

--- a/solution.py
+++ b/solution.py
@@ -47,7 +47,12 @@
         grad_own, master, first_moment, second_moment, clip_factor
     )
     rounded = new_master.astype(jnp.bfloat16)
-    tp_rows = lax.all_gather(rounded, "dp", axis=0, tiled=True)
+    ring = [rounded]
+    for hop in range(7):
+        ring.append(lax.ppermute(ring[-1], "dp", [(dev, (dev + 1) % 8) for dev in range(8)]))
+    tp_rows = jnp.roll(
+        jnp.concatenate(ring[::-1], axis=0), (lax.axis_index("dp") + 1) * ring[0].shape[0], axis=0
+    )
     return (new_master, new_first, new_second, tp_rows)
 
 

time: 626 us -> 693 us (1.11)
  waiting for transfers between devices: 444 us -> 483 us
  local copies, waits for them, and re-layouts: 85.4 us -> 114 us
    ppermute x0 -> x7, waiting for transfers between devices: none -> 169 us  [on_device(): lax.ppermute(ring[-1], 'dp', [(dev, (dev + 1) % 8) for dev in range(8)])]
    all_gather x1 -> x0, waiting for transfers between devices: 130 us -> none  [on_device(): tp_rows = lax.all_gather(rounded, 'dp', axis=0, tiled=True)]
    unnamed x7 -> x42, local copies, waits for them, and re-layouts: 85.4 us -> 106 us
    dynamic_slice x0 -> x1, local copies, waits for them, and re-layouts: none -> 6.96 us  [on_device(): jnp.roll(jnp.concatenate(ring[::-1], axis=0), (lax.axis_index('dp') + 1)...]
  transfers between devices with their start and end apart: 2 -> 8, of which waited for: 2 -> 8; matrix products, arithmetic and copies ran while one was open for 6% -> 5% of each run, Pallas kernels for 0% -> 0%
where the time goes in v1:
time: 693 us; the launch traced here: 691 us
  waiting for transfers between devices  483 us (70%)
  local copies, waits for them, and re-layouts  114 us (16%)
  blocking collectives  37.9 us (5%)
  matrix products  25.6 us (4%)
  other arithmetic  15.2 us (2%)
  between operations  14.9 us (2%)
    reduce_scatter x1, waiting for transfers between devices, reduce_rows(): lax.psum_scatter(jnp.einsum('ltr,ltc->rlc', layer_acts, layer_grads, pref...  314 us
    ppermute x7, waiting for transfers between devices, on_device(): lax.ppermute(ring[-1], 'dp', [(dev, (dev + 1) % 8) for dev in range(8)])  169 us
    unnamed x42, local copies, waits for them, and re-layouts  106 us
    psum x1, blocking collectives, on_device(): sum_squares = lax.psum(layer_sum, ('tp', 'dp'))  37.9 us
    dot_general x1, matrix products, reduce_rows(): jnp.einsum('ltr,ltc->rlc', layer_acts, layer_grads, preferred_element_typ...  25.6 us
  transfers between devices with their start and end apart: 8, of which 8 were waited for; matrix products, arithmetic and copies ran while one was open for 5% of the time, Pallas kernels for 0%

profile of v1, /device:TPU:0, one launch (start us, length us, event | category | flops | bytes accessed | tf_op | source)
XLA Modules:
  0.0 690.6 jit_solution(8069284192825838019)
XLA Ops:
  7.2 25.6 %convolution_bitcast_fusion = f32[2048,2,2048]{0,2,1:T(8,128)} fusion(bf16[2,1024,2048]{2,1,0:T(8,128)(2,1)} %param.6, bf16[2,1024,2048]{2,1,0:T(8,128)(2,1)} %param.5), kind=kOutput, calls=%fused_computation | convolution fusion | flops 17179869184 | bytes 50331648 | tf_op jit(solution)/shard_map/ltr,ltc->rlc/dot_general | solution.py:19
  32.9 7.2 %copy.13 = f32[256,2,2048]{0,2,1:T(8,128)} copy(f32[256,2,2048]{2,1,0:T(2,128)} %param.7) | data formatting | bytes 8388608 | tf_op args[2]
  40.1 7.2 %copy.9 = f32[256,2,2048]{0,2,1:T(8,128)} copy(f32[256,2,2048]{2,1,0:T(2,128)} %param.8) | data formatting | bytes 8388608 | tf_op args[3]
  47.3 313.9 %reduce-scatter.2.cloned.1.call-done = f32[256,2,2048]{0,2,1:T(8,128)} async-done(((f32[2048,2,2048]{0,2,1:T(8,128)}), f32[256,2,2048]{0,2,1:T(8,128)}) %reduce-scatter.2.cloned.1.call-update) | async-done | bytes 4194320 | tf_op jit(solution)/shard_map/reduce_scatter | solution.py:18
  361.2 3.9 multiply_reduce_fusion
  365.1 7.2 %copy.11 = f32[256,2,2048]{0,2,1:T(8,128)} copy(f32[256,2,2048]{2,1,0:T(2,128)} %param.9) | data formatting | bytes 8388608 | tf_op args[4]
  372.3 37.9 %psum.7 = f32[]{:T(128)} all-reduce(f32[]{:T(128)} %multiply_reduce_fusion), channel_id=1, replica_groups=mesh['tp'=4,'dp'=8] {'tp','dp'}, use_global_device_ids=true, to_apply=%region_2.0 | all-reduce | flops 1 | bytes 8 | tf_op jit(solution)/shard_map/psum | solution.py:40
  411.0 11.3 %fusion.1 = (bf16[256,2,2048]{0,2,1:T(8,128)(2,1)S(1)}, f32[256,2,2048]{0,2,1:T(8,128)}, f32[256,2,2048]{0,2,1:T(8,128)}, f32[256,2,2048]{0,2,1:T(8,128)}) fusion(f32[256,2,2048]{0,2,1:T(8,128)} %copy.13, f32[256,2,2048]{0,2,1:T(8,128)} %reduce-scatter.2.cloned.1.call-done, f32[]{:T(128)S(6)} %div.18, f32[256,2,2048]{0,2,1:T(8,128)} %copy.9, ...), kind=kLoop, calls=%fused_computation.23 | loop fusion | flops 17825792 | bytes 31457284 | tf_op jit(solution)/shard_map/convert_element_type | solution.py:49
  422.3 27.3 %collective-permute-done = bf16[256,2,2048]{0,2,1:T(8,128)(2,1)S(1)} collective-permute-done((bf16[256,2,2048]{0,2,1:T(8,128)(2,1)S(1)}, bf16[256,2,2048]{0,2,1:T(8,128)(2,1)S(1)}, u32[]{:S(2)}, u32[]{:S(2)}) %collective-permute-start) | collective-permute-done | bytes 2097184 | tf_op jit(solution)/shard_map/ppermute | solution.py:52
  450.9 27.3 %collective-permute-done.1 = bf16[256,2,2048]{0,2,1:T(8,128)(2,1)S(1)} collective-permute-done((bf16[256,2,2048]{0,2,1:T(8,128)(2,1)S(1)}, bf16[256,2,2048]{0,2,1:T(8,128)(2,1)S(1)}, u32[]{:S(2)}, u32[]{:S(2)}) %collective-permute-start.1) | collective-permute-done | bytes 2097184 | tf_op jit(solution)/shard_map/ppermute | solution.py:52
  479.5 27.3 %collective-permute-done.2 = bf16[256,2,2048]{0,2,1:T(8,128)(2,1)S(1)} collective-permute-done((bf16[256,2,2048]{0,2,1:T(8,128)(2,1)S(1)}, bf16[256,2,2048]{0,2,1:T(8,128)(2,1)S(1)}, u32[]{:S(2)}, u32[]{:S(2)}) %collective-permute-start.2) | collective-permute-done | bytes 2097184 | tf_op jit(solution)/shard_map/ppermute | solution.py:52
  508.1 27.3 %collective-permute-done.3 = bf16[256,2,2048]{0,2,1:T(8,128)(2,1)S(1)} collective-permute-done((bf16[256,2,2048]{0,2,1:T(8,128)(2,1)S(1)}, bf16[256,2,2048]{0,2,1:T(8,128)(2,1)S(1)}, u32[]{:S(2)}, u32[]{:S(2)}) %collective-permute-start.3) | collective-permute-done | bytes 2097184 | tf_op jit(solution)/shard_map/ppermute | solution.py:52
  536.7 27.3 %collective-permute-done.4 = bf16[256,2,2048]{0,2,1:T(8,128)(2,1)S(1)} collective-permute-done((bf16[256,2,2048]{0,2,1:T(8,128)(2,1)S(1)}, bf16[256,2,2048]{0,2,1:T(8,128)(2,1)S(1)}, u32[]{:S(2)}, u32[]{:S(2)}) %collective-permute-start.4) | collective-permute-done | bytes 2097184 | tf_op jit(solution)/shard_map/ppermute | solution.py:52
  565.3 27.4 %collective-permute-done.5 = bf16[256,2,2048]{0,2,1:T(8,128)(2,1)} collective-permute-done((bf16[256,2,2048]{0,2,1:T(8,128)(2,1)S(1)}, bf16[256,2,2048]{0,2,1:T(8,128)(2,1)}, u32[]{:S(2)}, u32[]{:S(2)}) %collective-permute-start.5) | collective-permute-done | bytes 2097184 | tf_op jit(solution)/shard_map/ppermute | solution.py:52
  592.6 7.3 %copy.14 = f32[256,2,2048]{2,1,0:T(2,128)} copy(f32[256,2,2048]{0,2,1:T(8,128)} %get-tuple-element.9) | data formatting | bytes 8388608
  599.9 7.3 %copy.15 = f32[256,2,2048]{2,1,0:T(2,128)} copy(f32[256,2,2048]{0,2,1:T(8,128)} %get-tuple-element.10) | data formatting | bytes 8388608
  607.2 7.3 %copy.16 = f32[256,2,2048]{2,1,0:T(2,128)} copy(f32[256,2,2048]{0,2,1:T(8,128)} %get-tuple-element.11) | data formatting | bytes 8388608
  614.5 5.7 collective-permute-done.6
  622.1 2.0 constant_dynamic-update-slice_fusion.14
  628.1 1.9 constant_dynamic-update-slice_fusion.7
  630.0 1.9 constant_dynamic-update-slice_fusion.6
  631.9 1.9 constant_dynamic-update-slice_fusion.5
  635.3 7.0 %constant_dynamic-slice_fusion = bf16[2048,2,2048]{0,2,1:T(8,128)(2,1)} fusion(bf16[4096,2,2048]{0,2,1:T(8,128)(2,1)S(1)} %constant_dynamic-update-slice_fusion, s32[]{:T(128)S(6)} %select_n.14), kind=kLoop, calls=%fused_computation.22 | loop fusion | bytes 33554436 | tf_op jit(solution)/shard_map/jit(_roll_dynamic)/dynamic_slice | solution.py:53
  642.3 41.5 %copy.17 = bf16[2048,2,2048]{2,1,0:T(2,128)(2,1)} copy(bf16[2048,2,2048]{0,2,1:T(8,128)(2,1)} %constant_dynamic-slice_fusion) | data formatting | bytes 33554432
  (41 shorter events, 14.0 us)
Async XLA Ops:
  7.2 354.1 %reduce-scatter.2.cloned.1.call-start = ((), (), s32[]{:S(2)}) async-start(), calls=%async_computation.1 | async-start | bytes 37748736 | tf_op jit(solution)/shard_map/reduce_scatter | solution.py:18
  422.3 27.3 %collective-permute-start = (bf16[256,2,2048]{0,2,1:T(8,128)(2,1)S(1)}, bf16[256,2,2048]{0,2,1:T(8,128)(2,1)S(1)}, u32[]{:S(2)}, u32[]{:S(2)}) collective-permute-start(bf16[256,2,2048]{0,2,1:T(8,128)(2,1)S(1)} %get-tuple-element.8), channel_id=1, source_target_pairs={{0,1},{1,2},{2,3},{3,4},{4,5},{5,6},{6,7},{7,0},{8,9},{9,10},{10,1... | collective-permute-start | bytes 6291464 | tf_op jit(solution)/shard_map/ppermute | solution.py:52
  449.6 1.3 copy-start
  450.9 27.3 %collective-permute-start.1 = (bf16[256,2,2048]{0,2,1:T(8,128)(2,1)S(1)}, bf16[256,2,2048]{0,2,1:T(8,128)(2,1)S(1)}, u32[]{:S(2)}, u32[]{:S(2)}) collective-permute-start(bf16[256,2,2048]{0,2,1:T(8,128)(2,1)S(1)} %collective-permute-done), channel_id=1, source_target_pairs={{0,1},{1,2},{2,3},{3,4},{4,5},{5,6},{6,7},{7,0},{8,9},{9,10},{10,1... | collective-permute-start | bytes 6291464 | tf_op jit(solution)/shard_map/ppermute | solution.py:52
  478.2 1.4 copy-start.2
  479.5 27.3 %collective-permute-start.2 = (bf16[256,2,2048]{0,2,1:T(8,128)(2,1)S(1)}, bf16[256,2,2048]{0,2,1:T(8,128)(2,1)S(1)}, u32[]{:S(2)}, u32[]{:S(2)}) collective-permute-start(bf16[256,2,2048]{0,2,1:T(8,128)(2,1)S(1)} %collective-permute-done.1), channel_id=1, source_target_pairs={{0,1},{1,2},{2,3},{3,4},{4,5},{5,6},{6,7},{7,0},{8,9},{9,10},{10,1... | collective-permute-start | bytes 6291464 | tf_op jit(solution)/shard_map/ppermute | solution.py:52
  506.8 1.3 copy-start.4
  508.1 27.3 %collective-permute-start.3 = (bf16[256,2,2048]{0,2,1:T(8,128)(2,1)S(1)}, bf16[256,2,2048]{0,2,1:T(8,128)(2,1)S(1)}, u32[]{:S(2)}, u32[]{:S(2)}) collective-permute-start(bf16[256,2,2048]{0,2,1:T(8,128)(2,1)S(1)} %collective-permute-done.2), channel_id=1, source_target_pairs={{0,1},{1,2},{2,3},{3,4},{4,5},{5,6},{6,7},{7,0},{8,9},{9,10},{10,1... | collective-permute-start | bytes 6291464 | tf_op jit(solution)/shard_map/ppermute | solution.py:52
  535.4 1.3 copy-start.6
  536.7 27.3 %collective-permute-start.4 = (bf16[256,2,2048]{0,2,1:T(8,128)(2,1)S(1)}, bf16[256,2,2048]{0,2,1:T(8,128)(2,1)S(1)}, u32[]{:S(2)}, u32[]{:S(2)}) collective-permute-start(bf16[256,2,2048]{0,2,1:T(8,128)(2,1)S(1)} %collective-permute-done.3), channel_id=1, source_target_pairs={{0,1},{1,2},{2,3},{3,4},{4,5},{5,6},{6,7},{7,0},{8,9},{9,10},{10,1... | collective-permute-start | bytes 6291464 | tf_op jit(solution)/shard_map/ppermute | solution.py:52
  563.9 1.3 copy-start.8
  565.3 27.4 %collective-permute-start.5 = (bf16[256,2,2048]{0,2,1:T(8,128)(2,1)S(1)}, bf16[256,2,2048]{0,2,1:T(8,128)(2,1)}, u32[]{:S(2)}, u32[]{:S(2)}) collective-permute-start(bf16[256,2,2048]{0,2,1:T(8,128)(2,1)S(1)} %collective-permute-done.4), channel_id=1, source_target_pairs={{0,1},{1,2},{2,3},{3,4},{4,5},{5,6},{6,7},{7,0},{8,9},{9,10},{10,1... | collective-permute-start | bytes 6291464 | tf_op jit(solution)/shard_map/ppermute | solution.py:52
  592.6 27.6 %collective-permute-start.6 = (bf16[256,2,2048]{0,2,1:T(8,128)(2,1)}, bf16[256,2,2048]{0,2,1:T(8,128)(2,1)}, u32[]{:S(2)}, u32[]{:S(2)}) collective-permute-start(bf16[256,2,2048]{0,2,1:T(8,128)(2,1)} %collective-permute-done.5), channel_id=1, source_target_pairs={{0,1},{1,2},{2,3},{3,4},{4,5},{5,6},{6,7},{7,0},{8,9},{9,10},{10,1... | collective-permute-start | bytes 6291464 | tf_op jit(solution)/shard_map/ppermute | solution.py:52
  614.5 9.6 %copy-start.9 = (bf16[256,2,2048]{0,2,1:T(8,128)(2,1)S(1)}, bf16[256,2,2048]{0,2,1:T(8,128)(2,1)}, u32[]{:S(2)}) copy-start(bf16[256,2,2048]{0,2,1:T(8,128)(2,1)} %copy-done.8) | copy-start | bytes 6291460
  622.1 2.4 copy-start.7
  624.2 1.6 copy-start.5
  624.5 2.0 copy-start.3
  625.8 1.7 copy-start.1
Sparse Core Ops, SparseCore 0:
  33.0 328.1 reduce-scatter.1
